TPU v7x, 32 devices: a whole 2x2x4 slice. The times are simulated.
32 devices in a mesh: node: 4 (over z), chip: 8 (over y, x, core).
Axes of the slice: x: 2, y: 2, z: 4, core: 2. Of those that a mesh axis runs over, the one named last changes fastest.
Arguments:
- pooled_grad: bfloat16 [2048, 4, 256], P(('node', 'chip')), may hold values from -6 to 6
- grad_scale: bfloat16 [2048, 4], P(('node', 'chip')), may hold values from 0.049804688 to 1
- hot_slot: int32 [2048, 4, 2], P(('node', 'chip')), may hold values from 0 to 511
- send_index: int32 [32, 32, 128], P(('node', 'chip')), may hold values from 0 to 255, as said below
- recv_row: int32 [32, 32, 128], P(('node', 'chip')), may hold values from 0 to 4096, as said below
- cold_weight: float32 [4, 32768, 256], P(None, ('node', 'chip')), may hold values from -3 to 3
- cold_accum: float32 [4, 32768], P(None, ('node', 'chip')), may hold values from 0.5 to 8
- hot_weight: float32 [4, 512, 256], replicated, may hold values from -3 to 3
- hot_accum: float32 [4, 512], replicated, may hold values from 1 to 64
Outputs:
- cold_weight_new: float32 [4, 32768, 256], P(None, ('node', 'chip'))
- cold_accum_new: float32 [4, 32768], P(None, ('node', 'chip'))
- hot_weight_new: float32 [4, 512, 256], replicated
- hot_accum_new: float32 [4, 512], replicated
Inputs may be any that keep to these rules, and one draw needn't show every extreme that they name: send_index and recv_row describe the same lookups: slot c from p to q is filled exactly when recv_row[q, p, c] < 4096, the filled slots of a pair come first, and the table in both entries agrees; some owners receive all 128 slots filled from every sender in every draw. `recv_row`: see send_index; empty slots hold 4096.
All inputs are finite; a program needn't handle non-finite values.
Results may differ from a plain program's by a relative error of at most 0.0003.
Values may be sent and summed in bfloat16 or wider, within the bound.
No kernel may reach another device: no remote copies, remote signals or barrier semaphores. Data moves between devices by JAX's collectives and lax.ppermute only.
A program may use at most 64 MiB of HBM per device.

v0:
```python
import math
import jax
import jax.numpy as jnp
from jax import lax
from jax.sharding import PartitionSpec as P

LEARN_RATE = 0.5


def adagrad(weight, accum, grad):
    accum_new = accum + jnp.mean(grad * grad, axis=-1)
    return (weight - LEARN_RATE * grad / jnp.sqrt(accum_new)[..., None], accum_new)


def per_device(
    pooled_grad,
    grad_scale,
    hot_slot,
    send_index,
    recv_row,
    cold_weight,
    cold_accum,
    hot_weight,
    hot_accum,
):
    b_dev, tables, width = pooled_grad.shape
    devices = send_index.shape[1]
    capacity = send_index.shape[2]
    source_rows = b_dev * tables
    pooled_rows = pooled_grad.reshape(source_rows, width)
    scale_rows = grad_scale.reshape(source_rows, 1)
    chosen = send_index.reshape(devices * capacity)
    selector = (chosen[:, None] == jnp.arange(source_rows, dtype=jnp.int32)[None, :]).astype(
        jnp.bfloat16
    )
    outgoing = jnp.dot(selector, pooled_rows, preferred_element_type=jnp.float32).astype(
        jnp.bfloat16
    )
    out_scale = (
        jnp.dot(selector, scale_rows, preferred_element_type=jnp.float32)
        .astype(jnp.bfloat16)
        .reshape(devices * capacity)
    )
    arrived, arrived_scale = (
        lax.all_to_all(
            outgoing.reshape(devices, capacity, width),
            ("node", "chip"),
            split_axis=0,
            concat_axis=0,
            tiled=True,
        ),
        lax.all_to_all(
            out_scale.reshape(devices, capacity),
            ("node", "chip"),
            split_axis=0,
            concat_axis=0,
            tiled=True,
        ),
    )
    slots = devices * capacity
    arrived_rows = arrived.reshape(slots, width)
    arrived_scale = arrived_scale.reshape(slots)
    targets = recv_row.reshape(slots)
    rows_dev = cold_weight.shape[1]
    local_rows = tables * rows_dev
    block = math.gcd(local_rows, 2048)
    blocks = local_rows // block

    def block_grad(first_row):
        levels = first_row + jnp.arange(block, dtype=jnp.int32)
        weights = jnp.where(
            levels[:, None] == targets[None, :], arrived_scale[None, :], jnp.zeros((), jnp.bfloat16)
        )
        return jnp.dot(weights, arrived_rows, preferred_element_type=jnp.float32)

    starts = jnp.arange(blocks, dtype=jnp.int32) * block
    cold_grad = lax.map(block_grad, starts).reshape(local_rows, width)
    new_weight, new_accum = adagrad(
        cold_weight.reshape(local_rows, width), cold_accum.reshape(local_rows), cold_grad
    )
    cold_weight_new = new_weight.reshape(tables, rows_dev, width)
    cold_accum_new = new_accum.reshape(tables, rows_dev)
    hot_rows = hot_weight.shape[1]
    levels = jnp.arange(hot_rows, dtype=jnp.int32)
    matches = jnp.sum((hot_slot[:, :, :, None] == levels).astype(jnp.float32), axis=2)
    coeffs = (matches * grad_scale.astype(jnp.float32)[:, :, None]).astype(jnp.bfloat16)
    hot_term = jnp.einsum("sth,std->thd", coeffs, pooled_grad, preferred_element_type=jnp.float32)
    hot_grad = lax.psum(hot_term, ("node", "chip"))
    hot_weight_new, hot_accum_new = adagrad(hot_weight, hot_accum, hot_grad)
    return (cold_weight_new, cold_accum_new, hot_weight_new, hot_accum_new)


def solution(mesh):
    placed = (
        P(("node", "chip"), None, None),
        P(("node", "chip"), None),
        P(("node", "chip"), None, None),
        P(("node", "chip"), None, None),
        P(("node", "chip"), None, None),
        P(None, ("node", "chip"), None),
        P(None, ("node", "chip")),
        P(),
        P(),
    )
    return jax.shard_map(
        per_device,
        mesh=mesh,
        in_specs=placed,
        out_specs=(P(None, ("node", "chip"), None), P(None, ("node", "chip")), P(), P()),
        check_vma=False,
    )
```

profile of v0, /device:TPU:0, one launch (start us, length us, event | category | flops | bytes accessed | tf_op | source)
XLA Modules:
  0.0 226.0 jit_solution(1676624236561834407)
XLA Ops:
  7.2 0.8 copy.25
  8.0 0.1 reshape.71
  8.1 1.7 fusion.8
  9.8 0.6 copy.26
  10.4 7.3 %all-to-all-start = ((bf16[32,1,128]{2,1,0:T(2,128)(2,1)}), bf16[32,1,128]{2,1,0:T(2,128)(2,1)S(1)}, u32[]{:S(2)}, u32[]{:S(2)}) async-start(bf16[32,1,128]{2,1,0:T(2,128)(2,1)} %copy.26), calls=%async_computation | async-start | bytes 32768 | tf_op jit(solution)/shard_map/all_to_all | solution.py:52
  17.7 0.9 reshape.68
  18.7 0.0 copy-start.5
  18.7 0.0 copy-start.4
  18.7 0.0 copy-start.1
  18.7 2.8 %convolution_convert_fusion = bf16[4096,256]{1,0:T(8,128)(2,1)} fusion(bf16[256,256]{1,0:T(8,128)(2,1)S(1)} %reshape.68, s32[4096]{0:T(1024)} %bitcast.35), kind=kOutput, calls=%fused_computation.10 | convolution fusion | flops 538968064 | bytes 2244608 | tf_op jit(solution)/shard_map/dot_general | solution.py:36
  21.5 3.4 %all-to-all-done = bf16[32,1,128]{2,1,0:T(2,128)(2,1)S(1)} async-done(((bf16[32,1,128]{2,1,0:T(2,128)(2,1)}), bf16[32,1,128]{2,1,0:T(2,128)(2,1)S(1)}, u32[]{:S(2)}, u32[]{:S(2)}) %all-to-all-start) | async-done | bytes 8224 | tf_op jit(solution)/shard_map/all_to_all | solution.py:52
  24.8 3.5 %all-to-all-start.1 = ((bf16[32,128,256]{2,1,0:T(8,128)(2,1)}), bf16[32,128,256]{2,1,0:T(8,128)(2,1)}, u32[]{:S(2)}, u32[]{:S(2)}) async-start(bf16[32,128,256]{2,1,0:T(8,128)(2,1)} %bitcast.7), calls=%async_computation.1 | async-start | bytes 4194304 | tf_op jit(solution)/shard_map/all_to_all | solution.py:45
  28.3 0.0 copy-start.3
  28.3 0.0 copy-start
  28.3 0.0 all-reduce.2.cloned.1.call-start
  28.4 0.2 convert_reduce_fusion
  28.6 1.9 fusion.11
  30.5 0.0 all-reduce.2.cloned.1.call-update
  30.6 153.3 %all-reduce.2.cloned.1.call-done = f32[4,512,256]{2,1,0:T(8,128)} async-done(((f32[4,512,256]{2,1,0:T(8,128)}), f32[4,512,256]{2,1,0:T(8,128)}) %all-reduce.2.cloned.1.call-update) | async-done | bytes 2097168 | tf_op jit(solution)/shard_map/psum | solution.py:88
  183.9 1.9 multiply_reduce_fusion.1
  185.9 0.6 fusion.14
  186.5 3.3 %divide_subtract_fusion.1 = f32[4,512,256]{2,1,0:T(8,128)} fusion(f32[4,512,256]{2,1,0:T(8,128)S(1)} %copy-done, f32[4,512,256]{2,1,0:T(8,128)} %all-reduce.2.cloned.1.call-done, f32[4,512]{1,0:T(4,128)S(1)} %get-tuple-element.49), kind=kLoop, calls=%fused_computation.15 | loop fusion | flops 1572864 | bytes 6299648 | tf_op jit(solution)/shard_map/sub | solution.py:12
  189.7 18.9 %while.10 = (s32[]{:T(128)}, f32[2,2048,256]{2,1,0:T(8,128)}, s32[2]{0:T(128)S(1)}, s32[1,32,128]{2,1,0:T(8,128)S(1)}, bf16[32,128]{1,0:T(8,128)(2,1)S(1)}, /*index=5*/bf16[4096,256]{1,0:T(8,128)(2,1)}, s32[]{:T(128)}) while((s32[]{:T(128)}, f32[2,2048,256]{2,1,0:T(8,128)}, s32[2]{0:T(128)S(1)}, s32[1,32,128]{2,1,0:T(8,128)S(1)}, ...), condition=%wide.region_1.2_spmd, body=%wide.region_0.1_spmd.sunk | while | flops 4311746560 | bytes 4235869 | solution.py:77
  189.7 0.6 dynamic_slice.5
  190.4 0.7 iota_add_fusion.2
  191.1 8.1 %fusion.22 = f32[2,2048,256]{2,1,0:T(8,128)} fusion(f32[2,2048,256]{2,1,0:T(8,128)} %get-tuple-element.100, s32[]{:T(128)} %get-tuple-element.99, bf16[4096,256]{1,0:T(8,128)(2,1)} %get-tuple-element.111, s32[4096]{0:T(1024)S(1)} %bitcast.36, s32[2048]{0:T(1024)S(1)} %iota_add_fusion.2, bf16[4096]{0:T(1024)(128)(2,1)S(1)} %bitcast.33), kind=kOutput, calls=%fused_computation.7.clone.1 | convolution fusion | flops 4311744512 | bytes 4227584 | tf_op jit(solution)/shard_map/while/body/eval_jaxpr/dot_general | solution.py:74
  199.2 0.6 dynamic_slice.5
  199.8 0.7 iota_add_fusion.2
  200.5 8.1 %fusion.22 = f32[2,2048,256]{2,1,0:T(8,128)} fusion(f32[2,2048,256]{2,1,0:T(8,128)} %get-tuple-element.100, s32[]{:T(128)} %get-tuple-element.99, bf16[4096,256]{1,0:T(8,128)(2,1)} %get-tuple-element.111, s32[4096]{0:T(1024)S(1)} %bitcast.36, s32[2048]{0:T(1024)S(1)} %iota_add_fusion.2, bf16[4096]{0:T(1024)(128)(2,1)S(1)} %bitcast.33), kind=kOutput, calls=%fused_computation.7.clone.1 | convolution fusion | flops 4311744512 | bytes 4227584 | tf_op jit(solution)/shard_map/while/body/eval_jaxpr/dot_general | solution.py:74
  208.6 4.7 %multiply_reduce_fusion = (f32[2,2048]{1,0:T(2,128)S(1)}, f32[2,2048,256]{2,1,0:T(8,128)}) fusion(f32[2,2048,256]{2,1,0:T(8,128)} %get-tuple-element.36), kind=kLoop, calls=%fused_computation.12 | loop fusion | flops 3141632 | bytes 8404992 | tf_op jit(solution)/shard_map/reduce_sum | solution.py:11
  213.4 0.6 fusion.15
  214.0 5.1 %divide_subtract_fusion = f32[4,1024,256]{2,1,0:T(8,128)} fusion(f32[4,1024,256]{2,1,0:T(8,128)} %param.16, f32[4,1024,256]{2,1,0:T(8,128)} %bitcast.30, f32[4,1024]{1,0:T(4,128)S(1)} %get-tuple-element.51), kind=kLoop, calls=%fused_computation.11 | loop fusion | flops 2097152 | bytes 12599296 | tf_op jit(solution)/shard_map/sub | solution.py:12
  (17 shorter events, 0.1 us)
Async XLA Ops:
  10.4 14.4 %all-to-all-start = ((bf16[32,1,128]{2,1,0:T(2,128)(2,1)}), bf16[32,1,128]{2,1,0:T(2,128)(2,1)S(1)}, u32[]{:S(2)}, u32[]{:S(2)}) async-start(bf16[32,1,128]{2,1,0:T(2,128)(2,1)} %copy.26), calls=%async_computation | async-start | bytes 32768 | tf_op jit(solution)/shard_map/all_to_all | solution.py:52
  18.7 9.7 %copy-start.5 = (bf16[64,4]{0,1:T(4,128)(2,1)S(1)}, bf16[64,4]{0,1:T(4,128)(2,1)}, u32[]{:S(2)}) copy-start(bf16[64,4]{0,1:T(4,128)(2,1)} %param.12) | copy-start | bytes 1540
  18.7 9.7 %copy-start.4 = (s32[64,4,2]{0,2,1:T(2,128)S(1)}, s32[64,4,2]{0,2,1:T(2,128)}, u32[]{:S(2)}) copy-start(s32[64,4,2]{0,2,1:T(2,128)} %param.13) | copy-start | bytes 6148
  18.7 9.9 %copy-start.1 = (bf16[64,4,256]{2,1,0:T(4,128)(2,1)S(1)}, bf16[64,4,256]{2,1,0:T(4,128)(2,1)}, u32[]{:S(2)}) copy-start(bf16[64,4,256]{2,1,0:T(4,128)(2,1)} %param.11) | copy-start | bytes 393220
  24.8 164.9 %all-to-all-start.1 = ((bf16[32,128,256]{2,1,0:T(8,128)(2,1)}), bf16[32,128,256]{2,1,0:T(8,128)(2,1)}, u32[]{:S(2)}, u32[]{:S(2)}) async-start(bf16[32,128,256]{2,1,0:T(8,128)(2,1)} %bitcast.7), calls=%async_computation.1 | async-start | bytes 4194304 | tf_op jit(solution)/shard_map/all_to_all | solution.py:45
  28.3 157.5 %copy-start.3 = (f32[4,512]{1,0:T(4,128)S(1)}, f32[4,512]{1,0:T(4,128)}, u32[]{:S(2)}) copy-start(f32[4,512]{1,0:T(4,128)} %param.19) | copy-start | bytes 24580
  28.3 158.1 %copy-start = (f32[4,512,256]{2,1,0:T(8,128)S(1)}, f32[4,512,256]{2,1,0:T(8,128)}, u32[]{:S(2)}) copy-start(f32[4,512,256]{2,1,0:T(8,128)} %param.18) | copy-start | bytes 6291460
  28.3 155.6 %all-reduce.2.cloned.1.call-start = ((), (), s32[]{:S(2)}) async-start(), calls=%async_computation.2 | async-start | bytes 4194304 | tf_op jit(solution)/shard_map/psum | solution.py:88
  30.6 159.1 %copy-start.6 = (s32[1,32,128]{2,1,0:T(8,128)S(1)}, s32[1,32,128]{2,1,0:T(8,128)}, u32[]{:S(2)}) copy-start(s32[1,32,128]{2,1,0:T(8,128)} %param.15) | copy-start | bytes 49156
  208.6 4.8 %copy-start.2 = (f32[4,1024]{1,0:T(4,128)S(1)}, f32[4,1024]{1,0:T(4,128)}, u32[]{:S(2)}) copy-start(f32[4,1024]{1,0:T(4,128)} %param.17) | copy-start | bytes 49156
Sparse Core Ops, SparseCore 0:
  35.1 148.7 all-reduce.1
where the time goes:
time: 226 us
  waiting for transfers between devices  157 us (69%)
  matrix products  22.6 us (10%)
  other arithmetic  17.8 us (8%)
  between operations  14.2 us (6%)
  starting transfers between devices  10.9 us (5%)
  local copies, waits for them, and re-layouts  3.84 us (2%)
    psum x1, waiting for transfers between devices, per_device(): hot_grad = lax.psum(hot_term, ('node', 'chip'))  153 us
    dot_general x2, matrix products, block_grad(): return jnp.dot(weights, arrived_rows, preferred_element_type=jnp.float32)  16.2 us
    sub x2, other arithmetic, adagrad(): weight - LEARN_RATE * grad / jnp.sqrt(accum_new)[..., None]  8.39 us
    all_to_all x1, starting transfers between devices, per_device(): lax.all_to_all(out_scale.reshape(devices, capacity), ('node', 'chip'), sp...  7.33 us
    reduce_sum x2, other arithmetic, adagrad(): accum_new = accum + jnp.mean(grad * grad, axis=-1)  6.65 us
  transfers between devices with their start and end apart: 3, of which 2 were waited for; matrix products, arithmetic and copies ran while one was open for 5% of the time, Pallas kernels for 0%

commit v1 on v0

--- a/solution.py
+++ b/solution.py
@@ -5,6 +5,11 @@
 from jax.sharding import PartitionSpec as P
 
 LEARN_RATE = 0.5
+
+
+def _play_paths(x_local):
+    moved = lax.psum(x_local, axis_name="chip")
+    return lax.psum(moved, axis_name="node")
 
 
 def adagrad(weight, accum, grad):
@@ -85,7 +90,7 @@
     matches = jnp.sum((hot_slot[:, :, :, None] == levels).astype(jnp.float32), axis=2)
     coeffs = (matches * grad_scale.astype(jnp.float32)[:, :, None]).astype(jnp.bfloat16)
     hot_term = jnp.einsum("sth,std->thd", coeffs, pooled_grad, preferred_element_type=jnp.float32)
-    hot_grad = lax.psum(hot_term, ("node", "chip"))
+    hot_grad = _play_paths(hot_term)
     hot_weight_new, hot_accum_new = adagrad(hot_weight, hot_accum, hot_grad)
     return (cold_weight_new, cold_accum_new, hot_weight_new, hot_accum_new)
 

time: 226 us -> 236 us (1.044)
  waiting for transfers between devices: 157 us -> 166 us
    psum x1 -> x2, waiting for transfers between devices: 153 us -> 163 us  [the longest x1 87.5 us: _play_paths(): return lax.psum(moved, axis_name='node')]
  transfers between devices with their start and end apart: 3 -> 4, of which waited for: 2 -> 3; matrix products, arithmetic and copies ran while one was open for 5% -> 5% of each run, Pallas kernels for 0% -> 0%
where the time goes in v1:
time: 236 us
  waiting for transfers between devices  166 us (70%)
  matrix products  22.6 us (10%)
  other arithmetic  17.8 us (8%)
  between operations  14.2 us (6%)
  starting transfers between devices  10.9 us (5%)
  local copies, waits for them, and re-layouts  3.89 us (2%)
    psum x1, waiting for transfers between devices, _play_paths(): return lax.psum(moved, axis_name='node')  87.5 us
    psum x1, waiting for transfers between devices, _play_paths(): moved = lax.psum(x_local, axis_name='chip')  75.7 us
    dot_general x2, matrix products, block_grad(): return jnp.dot(weights, arrived_rows, preferred_element_type=jnp.float32)  16.2 us
    sub x2, other arithmetic, adagrad(): weight - LEARN_RATE * grad / jnp.sqrt(accum_new)[..., None]  8.39 us
    all_to_all x1, starting transfers between devices, per_device(): lax.all_to_all(out_scale.reshape(devices, capacity), ('node', 'chip'), sp...  7.33 us
    reduce_sum x2, other arithmetic, adagrad(): accum_new = accum + jnp.mean(grad * grad, axis=-1)  6.65 us
  transfers between devices with their start and end apart: 4, of which 3 were waited for; matrix products, arithmetic and copies ran while one was open for 5% of the time, Pallas kernels for 0%

profile of v1, /device:TPU:0, one launch (start us, length us, event | category | flops | bytes accessed | tf_op | source)
XLA Modules:
  0.0 235.9 jit_solution(4738555439074217519)
XLA Ops:
  7.2 0.8 copy.25
  8.0 0.1 reshape.71
  8.1 1.7 fusion.8
  9.8 0.6 copy.26
  10.5 7.3 %all-to-all-start = ((bf16[32,1,128]{2,1,0:T(2,128)(2,1)}), bf16[32,1,128]{2,1,0:T(2,128)(2,1)S(1)}, u32[]{:S(2)}, u32[]{:S(2)}) async-start(bf16[32,1,128]{2,1,0:T(2,128)(2,1)} %copy.26), calls=%async_computation | async-start | bytes 32768 | tf_op jit(solution)/shard_map/all_to_all | solution.py:57
  17.8 0.9 reshape.68
  18.7 0.0 copy-start.1
  18.8 2.8 %convolution_convert_fusion = bf16[4096,256]{1,0:T(8,128)(2,1)} fusion(bf16[256,256]{1,0:T(8,128)(2,1)S(1)} %reshape.68, s32[4096]{0:T(1024)} %bitcast.35), kind=kOutput, calls=%fused_computation.10 | convolution fusion | flops 538968064 | bytes 2244608 | tf_op jit(solution)/shard_map/dot_general | solution.py:41
  21.5 0.2 convert_reduce_fusion
  21.7 3.2 %all-to-all-done = bf16[32,1,128]{2,1,0:T(2,128)(2,1)S(1)} async-done(((bf16[32,1,128]{2,1,0:T(2,128)(2,1)}), bf16[32,1,128]{2,1,0:T(2,128)(2,1)S(1)}, u32[]{:S(2)}, u32[]{:S(2)}) %all-to-all-start) | async-done | bytes 8224 | tf_op jit(solution)/shard_map/all_to_all | solution.py:57
  24.9 3.5 %all-to-all-start.1 = ((bf16[32,128,256]{2,1,0:T(8,128)(2,1)}), bf16[32,128,256]{2,1,0:T(8,128)(2,1)}, u32[]{:S(2)}, u32[]{:S(2)}) async-start(bf16[32,128,256]{2,1,0:T(8,128)(2,1)} %bitcast.7), calls=%async_computation.1 | async-start | bytes 4194304 | tf_op jit(solution)/shard_map/all_to_all | solution.py:50
  28.4 0.0 all-reduce.3.cloned.1.call-start
  28.5 1.9 fusion.11
  30.4 0.0 all-reduce.3.cloned.1.call-update
  30.4 0.0 all-reduce.5.cloned.1.call-start
  30.5 75.7 %all-reduce.3.cloned.1.call-done = f32[4,512,256]{2,1,0:T(8,128)} async-done(((f32[4,512,256]{2,1,0:T(8,128)}), f32[4,512,256]{2,1,0:T(8,128)}) %all-reduce.3.cloned.1.call-update) | async-done | bytes 2097168 | tf_op jit(solution)/shard_map/psum | solution.py:11
  106.2 0.0 all-reduce.5.cloned.1.call-update
  106.3 0.0 copy-start.6
  106.3 87.5 %all-reduce.5.cloned.1.call-done = f32[4,512,256]{2,1,0:T(8,128)} async-done(((f32[4,512,256]{2,1,0:T(8,128)}), f32[4,512,256]{2,1,0:T(8,128)}) %all-reduce.5.cloned.1.call-update) | async-done | bytes 2097168 | tf_op jit(solution)/shard_map/psum | solution.py:12
  193.8 1.9 multiply_reduce_fusion.1
  195.8 0.6 fusion.14
  196.4 3.3 %divide_subtract_fusion.1 = f32[4,512,256]{2,1,0:T(8,128)} fusion(f32[4,512,256]{2,1,0:T(8,128)S(1)} %copy-done, f32[4,512,256]{2,1,0:T(8,128)} %all-reduce.5.cloned.1.call-done, f32[4,512]{1,0:T(4,128)S(1)} %get-tuple-element.49), kind=kLoop, calls=%fused_computation.15 | loop fusion | flops 1572864 | bytes 6299648 | tf_op jit(solution)/shard_map/sub | solution.py:17
  199.6 18.9 %while.10 = (s32[]{:T(128)}, f32[2,2048,256]{2,1,0:T(8,128)}, s32[2]{0:T(128)S(1)}, s32[1,32,128]{2,1,0:T(8,128)S(1)}, bf16[32,128]{1,0:T(8,128)(2,1)S(1)}, /*index=5*/bf16[4096,256]{1,0:T(8,128)(2,1)}, s32[]{:T(128)}) while((s32[]{:T(128)}, f32[2,2048,256]{2,1,0:T(8,128)}, s32[2]{0:T(128)S(1)}, s32[1,32,128]{2,1,0:T(8,128)S(1)}, ...), condition=%wide.region_1.2_spmd, body=%wide.region_0.1_spmd.sunk | while | flops 4311746560 | bytes 4235869 | solution.py:82
  199.6 0.6 dynamic_slice.5
  200.3 0.7 iota_add_fusion.2
  201.0 8.1 %fusion.22 = f32[2,2048,256]{2,1,0:T(8,128)} fusion(f32[2,2048,256]{2,1,0:T(8,128)} %get-tuple-element.100, s32[]{:T(128)} %get-tuple-element.99, bf16[4096,256]{1,0:T(8,128)(2,1)} %get-tuple-element.111, s32[4096]{0:T(1024)S(1)} %bitcast.36, s32[2048]{0:T(1024)S(1)} %iota_add_fusion.2, bf16[4096]{0:T(1024)(128)(2,1)S(1)} %bitcast.33), kind=kOutput, calls=%fused_computation.7.clone.1 | convolution fusion | flops 4311744512 | bytes 4227584 | tf_op jit(solution)/shard_map/while/body/eval_jaxpr/dot_general | solution.py:79
  209.1 0.6 dynamic_slice.5
  209.7 0.7 iota_add_fusion.2
  210.4 8.1 %fusion.22 = f32[2,2048,256]{2,1,0:T(8,128)} fusion(f32[2,2048,256]{2,1,0:T(8,128)} %get-tuple-element.100, s32[]{:T(128)} %get-tuple-element.99, bf16[4096,256]{1,0:T(8,128)(2,1)} %get-tuple-element.111, s32[4096]{0:T(1024)S(1)} %bitcast.36, s32[2048]{0:T(1024)S(1)} %iota_add_fusion.2, bf16[4096]{0:T(1024)(128)(2,1)S(1)} %bitcast.33), kind=kOutput, calls=%fused_computation.7.clone.1 | convolution fusion | flops 4311744512 | bytes 4227584 | tf_op jit(solution)/shard_map/while/body/eval_jaxpr/dot_general | solution.py:79
  218.5 4.7 %multiply_reduce_fusion = (f32[2,2048]{1,0:T(2,128)S(1)}, f32[2,2048,256]{2,1,0:T(8,128)}) fusion(f32[2,2048,256]{2,1,0:T(8,128)} %get-tuple-element.36), kind=kLoop, calls=%fused_computation.12 | loop fusion | flops 3141632 | bytes 8404992 | tf_op jit(solution)/shard_map/reduce_sum | solution.py:16
  223.3 0.6 fusion.15
  223.9 5.1 %divide_subtract_fusion = f32[4,1024,256]{2,1,0:T(8,128)} fusion(f32[4,1024,256]{2,1,0:T(8,128)} %param.16, f32[4,1024,256]{2,1,0:T(8,128)} %bitcast.30, f32[4,1024]{1,0:T(4,128)S(1)} %get-tuple-element.51), kind=kLoop, calls=%fused_computation.11 | loop fusion | flops 2097152 | bytes 12599296 | tf_op jit(solution)/shard_map/sub | solution.py:17
  (20 shorter events, 0.1 us)
Async XLA Ops:
  7.2 14.5 %copy-start.5 = (bf16[64,4]{0,1:T(4,128)(2,1)S(1)}, bf16[64,4]{0,1:T(4,128)(2,1)}, u32[]{:S(2)}) copy-start(bf16[64,4]{0,1:T(4,128)(2,1)} %param.12) | copy-start | bytes 1540
  7.2 14.3 %copy-start.4 = (s32[64,4,2]{0,2,1:T(2,128)S(1)}, s32[64,4,2]{0,2,1:T(2,128)}, u32[]{:S(2)}) copy-start(s32[64,4,2]{0,2,1:T(2,128)} %param.13) | copy-start | bytes 6148
  10.5 14.4 %all-to-all-start = ((bf16[32,1,128]{2,1,0:T(2,128)(2,1)}), bf16[32,1,128]{2,1,0:T(2,128)(2,1)S(1)}, u32[]{:S(2)}, u32[]{:S(2)}) async-start(bf16[32,1,128]{2,1,0:T(2,128)(2,1)} %copy.26), calls=%async_computation | async-start | bytes 32768 | tf_op jit(solution)/shard_map/all_to_all | solution.py:57
  18.7 9.7 %copy-start.1 = (bf16[64,4,256]{2,1,0:T(4,128)(2,1)S(1)}, bf16[64,4,256]{2,1,0:T(4,128)(2,1)}, u32[]{:S(2)}) copy-start(bf16[64,4,256]{2,1,0:T(4,128)(2,1)} %param.11) | copy-start | bytes 393220
  24.9 174.7 %all-to-all-start.1 = ((bf16[32,128,256]{2,1,0:T(8,128)(2,1)}), bf16[32,128,256]{2,1,0:T(8,128)(2,1)}, u32[]{:S(2)}, u32[]{:S(2)}) async-start(bf16[32,128,256]{2,1,0:T(8,128)(2,1)} %bitcast.7), calls=%async_computation.1 | async-start | bytes 4194304 | tf_op jit(solution)/shard_map/all_to_all | solution.py:50
  28.4 167.4 %copy-start.3 = (f32[4,512]{1,0:T(4,128)S(1)}, f32[4,512]{1,0:T(4,128)}, u32[]{:S(2)}) copy-start(f32[4,512]{1,0:T(4,128)} %param.19) | copy-start | bytes 24580
  28.4 168.0 %copy-start = (f32[4,512,256]{2,1,0:T(8,128)S(1)}, f32[4,512,256]{2,1,0:T(8,128)}, u32[]{:S(2)}) copy-start(f32[4,512,256]{2,1,0:T(8,128)} %param.18) | copy-start | bytes 6291460
  28.4 77.8 %all-reduce.3.cloned.1.call-start = ((), (), s32[]{:S(2)}) async-start(), calls=%async_computation.2 | async-start | bytes 4194304 | tf_op jit(solution)/shard_map/psum | solution.py:11
  30.4 163.4 %all-reduce.5.cloned.1.call-start = ((), (), s32[]{:S(2)}) async-start(), calls=%async_computation.3 | async-start | bytes 4194304 | tf_op jit(solution)/shard_map/psum | solution.py:12
  106.3 93.4 %copy-start.6 = (s32[1,32,128]{2,1,0:T(8,128)S(1)}, s32[1,32,128]{2,1,0:T(8,128)}, u32[]{:S(2)}) copy-start(s32[1,32,128]{2,1,0:T(8,128)} %param.15) | copy-start | bytes 49156
  218.5 4.8 %copy-start.2 = (f32[4,1024]{1,0:T(4,128)S(1)}, f32[4,1024]{1,0:T(4,128)}, u32[]{:S(2)}) copy-start(f32[4,1024]{1,0:T(4,128)} %param.17) | copy-start | bytes 49156
Sparse Core Ops, SparseCore 0:
  33.0 73.1 all-reduce.2
  108.6 85.1 all-reduce.4
